TPU v7x, 256 devices: a whole 4x4x8 slice. The times are simulated.
256 devices in a mesh: vert: 16 (over x, y), feat: 16 (over z, core).
Axes of the slice: x: 4, y: 4, z: 8, core: 2. Of those that a mesh axis runs over, the one named last changes fastest.
Arguments:
- features: bfloat16 [131072, 256], P('vert', 'feat'), may hold values from -6 to 6
- tiles: bfloat16 [1024, 16, 128, 128], P('vert'), may hold values from -0.1875 to 0.1875
- tile_cols: int32 [1024, 16], P('vert'), may hold values from 0 to 127
- tile_count: int32 [1024], P('vert'), may hold values from 1 to 16, as said below
- send_list: int32 [16, 16, 4], P('vert'), may hold values from 0 to 63
- weight: bfloat16 [256, 256], replicated, may hold values from -0.375 to 0.375
- bias: float32 [256], replicated, may hold values from -3 to 3
Outputs:
- node_out: bfloat16 [131072, 256], P(('vert', 'feat'))
Inputs may be any that keep to these rules, and one draw needn't show every extreme that they name: Row block r uses tile places 0 to tile_count[r] - 1; in every draw some row block uses all 16.
All inputs are finite; a program needn't handle non-finite values.
Results may differ from a plain program's by a relative error of at most 0.0044.
Values may be sent and summed in bfloat16 or wider, within the bound.
No kernel may reach another device: no remote copies, remote signals or barrier semaphores. Data moves between devices by JAX's collectives and lax.ppermute only.
A program may use at most 128 MiB of HBM per device.

v0:
```python
import jax
import jax.numpy as jnp
from jax import lax
from jax.sharding import PartitionSpec as P


def add_tile(total, extended, tiles, tile_cols, tile_count, tile_slot):
    wanted = lax.dynamic_index_in_dim(tile_cols, tile_slot, 1, keepdims=False)
    picked = jnp.take(extended, wanted, axis=0)
    tile_page = lax.dynamic_index_in_dim(tiles, tile_slot, 1, keepdims=False)
    product = jnp.einsum("rcj,rij->cri", picked, tile_page, preferred_element_type=jnp.float32)
    is_live = tile_slot < tile_count
    return total + jnp.where(is_live[None, :, None], product, jnp.float32(0.0))


def per_device(features, tiles, tile_cols, tile_count, send_list, weight, bias):
    block_count = tiles.shape[0]
    tile_depth = tiles.shape[1]
    edge = tiles.shape[2]
    width = features.shape[1]
    vert_count = lax.axis_size("vert")
    slot_count = send_list.shape[2]
    blocks = jnp.transpose(features.reshape(block_count, edge, width), (0, 2, 1))
    chosen = jnp.take(blocks, send_list[0], axis=0)
    arrived = lax.all_to_all(chosen, "vert", split_axis=0, concat_axis=0, tiled=True)
    extended = jnp.concatenate(
        [blocks, arrived.reshape(vert_count * slot_count, width, edge)], axis=0
    )
    total = jnp.zeros((width, block_count, edge), jnp.float32)
    for tile_slot in range(tile_depth):
        total = add_tile(total, extended, tiles, tile_cols, tile_count, tile_slot)
    hidden = total.astype(jnp.bfloat16).reshape(width, block_count * edge)
    full_rows = lax.all_to_all(hidden, "feat", split_axis=1, concat_axis=0, tiled=True)
    mixed_rows = lax.dot_general(
        full_rows, weight, (((0,), (0,)), ((), ())), preferred_element_type=jnp.float32
    )
    return jnp.maximum(mixed_rows + bias, jnp.float32(0.0)).astype(jnp.bfloat16)


def solution(mesh):
    return jax.shard_map(
        per_device,
        mesh=mesh,
        in_specs=(
            P("vert", "feat"),
            P("vert", None, None, None),
            P("vert", None),
            P("vert"),
            P("vert", None, None),
            P(),
            P(),
        ),
        out_specs=P(("vert", "feat"), None),
        check_vma=False,
    )
```

profile of v0, /device:TPU:1, one launch (start us, length us, event | category | flops | bytes accessed | tf_op | source)
XLA Modules:
  0.0 102.2 jit_solution(15791302507142877693)
XLA Ops:
  0.0 0.7 compare_select_fusion
  0.7 0.7 compare_and_fusion.16
  1.5 0.1 copy.69
  1.6 0.1 reshape.199
  1.7 0.1 copy.68
  1.8 0.6 gather_fusion
  2.4 0.8 broadcast_select_fusion
  3.2 7.6 %all-to-all-start = ((bf16[16,4,16,128]{3,2,1,0:T(8,128)(2,1)}), bf16[16,4,16,128]{3,2,1,0:T(8,128)(2,1)S(1)}, u32[]{:S(2)}, u32[]{:S(2)}) async-start(bf16[16,4,16,128]{3,2,1,0:T(8,128)(2,1)} %broadcast_select_fusion), calls=%async_computation | async-start | bytes 524288 | tf_op jit(solution)/shard_map/all_to_all | solution.py:25
  10.8 1.1 %compare_and_fusion = (pred[64]{0:T(512)(128)(4,1)S(1)}, s32[64]{0:T(128)S(1)}, pred[64]{0:T(512)(128)(4,1)S(1)}, s32[64]{0:T(128)S(1)}, pred[64]{0:T(512)(128)(...) fusion(s32[64,16]{0,1:T(8,128)} %param.11), kind=kLoop, calls=%fused_computation.187 | loop fusion | flops 6144 | bytes 9216 | tf_op jit(solution)/shard_map/jit(_take)/and | solution.py:9
  12.0 0.7 broadcast_compare_fusion
  12.7 5.6 %all-to-all-done = bf16[16,4,16,128]{3,2,1,0:T(8,128)(2,1)S(1)} async-done(((bf16[16,4,16,128]{3,2,1,0:T(8,128)(2,1)}), bf16[16,4,16,128]{3,2,1,0:T(8,128)(2,1)S(1)}, u32[]{:S(2)}, u32[]{:S(2)}) %all-to-all-start) | async-done | bytes 262176 | tf_op jit(solution)/shard_map/all_to_all | solution.py:25
  18.3 1.3 %gather_fusion.1 = bf16[64,16,128]{2,1,0:T(8,128)(2,1)} fusion(bf16[128,16,128]{2,1,0:T(8,128)(2,1)S(1)} %pad_maximum_fusion, s32[1024]{0:T(1024)S(1)} %get-tuple-element.99), kind=kCustom, calls=%fused_computation.clone | custom fusion | bytes 524544 | tf_op jit(solution)/shard_map/jit(_take)/gather | solution.py:9
  19.6 1.3 %gather_fusion.2 = bf16[64,16,128]{2,1,0:T(8,128)(2,1)} fusion(bf16[128,16,128]{2,1,0:T(8,128)(2,1)S(1)} %pad_maximum_fusion, s32[1024]{0:T(1024)S(1)} %get-tuple-element.98), kind=kCustom, calls=%fused_computation.1.clone | custom fusion | bytes 524544 | tf_op jit(solution)/shard_map/jit(_take)/gather | solution.py:9
  21.0 1.3 %gather_fusion.3 = bf16[64,16,128]{2,1,0:T(8,128)(2,1)} fusion(bf16[128,16,128]{2,1,0:T(8,128)(2,1)S(1)} %pad_maximum_fusion, s32[1024]{0:T(1024)S(1)} %get-tuple-element.97), kind=kCustom, calls=%fused_computation.2.clone | custom fusion | bytes 524544 | tf_op jit(solution)/shard_map/jit(_take)/gather | solution.py:9
  22.3 1.3 %gather_fusion.4 = bf16[64,16,128]{2,1,0:T(8,128)(2,1)} fusion(bf16[128,16,128]{2,1,0:T(8,128)(2,1)S(1)} %pad_maximum_fusion, s32[1024]{0:T(1024)S(1)} %get-tuple-element.96), kind=kCustom, calls=%fused_computation.3.clone | custom fusion | bytes 524544 | tf_op jit(solution)/shard_map/jit(_take)/gather | solution.py:9
  23.6 1.3 %gather_fusion.5 = bf16[64,16,128]{2,1,0:T(8,128)(2,1)} fusion(bf16[128,16,128]{2,1,0:T(8,128)(2,1)S(1)} %pad_maximum_fusion, s32[1024]{0:T(1024)S(1)} %get-tuple-element.95), kind=kCustom, calls=%fused_computation.4.clone | custom fusion | bytes 524544 | tf_op jit(solution)/shard_map/jit(_take)/gather | solution.py:9
  25.0 1.3 %gather_fusion.6 = bf16[64,16,128]{2,1,0:T(8,128)(2,1)} fusion(bf16[128,16,128]{2,1,0:T(8,128)(2,1)S(1)} %pad_maximum_fusion, s32[1024]{0:T(1024)S(1)} %get-tuple-element.94), kind=kCustom, calls=%fused_computation.5.clone | custom fusion | bytes 524544 | tf_op jit(solution)/shard_map/jit(_take)/gather | solution.py:9
  26.3 0.6 gather_fusion.7
  26.9 0.6 gather_fusion.8
  27.6 0.6 gather_fusion.9
  28.2 0.6 gather_fusion.10
  28.8 0.6 gather_fusion.11
  29.5 0.6 gather_fusion.12
  30.1 0.6 gather_fusion.13
  30.7 0.6 gather_fusion.14
  31.4 0.6 gather_fusion.15
  32.0 0.6 gather_fusion.16
  32.7 3.0 %fusion.48 = f32[64,16,128]{2,1,0:T(8,128)S(1)} fusion(bf16[64,16,128,128]{3,2,1,0:T(8,128)(2,1)} %param.10, bf16[64,16,128]{2,1,0:T(8,128)(2,1)} %gather_fusion.1, pred[64]{0:T(512)(128)(4,1)S(1)} %get-tuple-element.64, pred[64]{0:T(512)(128)(4,1)S(1)} %get-tuple-element.82), kind=kOutput, calls=%fused_computation.65 | convolution fusion | flops 33816576 | bytes 2883712 | tf_op jit(solution)/shard_map/rcj,rij->cri/dot_general | solution.py:11
  35.6 2.9 %fusion.141 = f32[64,16,128]{2,1,0:T(8,128)S(1)} fusion(f32[64,16,128]{2,1,0:T(8,128)S(1)} %fusion.48, bf16[64,16,128,128]{3,2,1,0:T(8,128)(2,1)} %param.10, bf16[64,16,128]{2,1,0:T(8,128)(2,1)} %gather_fusion.2, pred[64]{0:T(512)(128)(4,1)S(1)} %get-tuple-element.62, pred[64]{0:T(512)(128)(4,1)S(1)} %get-tuple-element.81), kind=kOutput, calls=%fused_computation.96 | convolution fusion | flops 33947648 | bytes 3408000 | tf_op jit(solution)/shard_map/rcj,rij->cri/dot_general | solution.py:11
  38.6 2.9 %fusion.138 = f32[64,16,128]{2,1,0:T(8,128)S(1)} fusion(f32[64,16,128]{2,1,0:T(8,128)S(1)} %fusion.141, bf16[64,16,128,128]{3,2,1,0:T(8,128)(2,1)} %param.10, bf16[64,16,128]{2,1,0:T(8,128)(2,1)} %gather_fusion.3, pred[64]{0:T(512)(128)(4,1)S(1)} %get-tuple-element.60, pred[64]{0:T(512)(128)(4,1)S(1)} %get-tuple-element.80), kind=kOutput, calls=%fused_computation.95 | convolution fusion | flops 33947648 | bytes 3408000 | tf_op jit(solution)/shard_map/rcj,rij->cri/dot_general | solution.py:11
  41.5 2.9 %fusion.135 = f32[64,16,128]{2,1,0:T(8,128)S(1)} fusion(f32[64,16,128]{2,1,0:T(8,128)S(1)} %fusion.138, bf16[64,16,128,128]{3,2,1,0:T(8,128)(2,1)} %param.10, bf16[64,16,128]{2,1,0:T(8,128)(2,1)} %gather_fusion.4, pred[64]{0:T(512)(128)(4,1)S(1)} %get-tuple-element.58, pred[64]{0:T(512)(128)(4,1)S(1)} %get-tuple-element.79), kind=kOutput, calls=%fused_computation.94 | convolution fusion | flops 33947648 | bytes 3408000 | tf_op jit(solution)/shard_map/rcj,rij->cri/dot_general | solution.py:11
  44.5 2.9 %fusion.132 = f32[64,16,128]{2,1,0:T(8,128)S(1)} fusion(f32[64,16,128]{2,1,0:T(8,128)S(1)} %fusion.135, bf16[64,16,128,128]{3,2,1,0:T(8,128)(2,1)} %param.10, bf16[64,16,128]{2,1,0:T(8,128)(2,1)} %gather_fusion.5, pred[64]{0:T(512)(128)(4,1)S(1)} %get-tuple-element.56, pred[64]{0:T(512)(128)(4,1)S(1)} %get-tuple-element.78), kind=kOutput, calls=%fused_computation.93 | convolution fusion | flops 33947648 | bytes 3408000 | tf_op jit(solution)/shard_map/rcj,rij->cri/dot_general | solution.py:11
  47.4 2.9 %fusion.129 = f32[64,16,128]{2,1,0:T(8,128)S(1)} fusion(f32[64,16,128]{2,1,0:T(8,128)S(1)} %fusion.132, bf16[64,16,128,128]{3,2,1,0:T(8,128)(2,1)} %param.10, bf16[64,16,128]{2,1,0:T(8,128)(2,1)} %gather_fusion.6, pred[64]{0:T(512)(128)(4,1)S(1)} %get-tuple-element.54, pred[64]{0:T(512)(128)(4,1)S(1)} %get-tuple-element.77), kind=kOutput, calls=%fused_computation.92 | convolution fusion | flops 33947648 | bytes 3408000 | tf_op jit(solution)/shard_map/rcj,rij->cri/dot_general | solution.py:11
  50.3 2.9 %fusion.126 = f32[64,16,128]{2,1,0:T(8,128)S(1)} fusion(f32[64,16,128]{2,1,0:T(8,128)S(1)} %fusion.129, bf16[64,16,128,128]{3,2,1,0:T(8,128)(2,1)} %param.10, bf16[64,16,128]{2,1,0:T(8,128)(2,1)S(1)} %gather_fusion.7, pred[64]{0:T(512)(128)(4,1)S(1)} %get-tuple-element.52, pred[64]{0:T(512)(128)(4,1)S(1)} %get-tuple-element.76), kind=kOutput, calls=%fused_computation.91 | convolution fusion | flops 33947648 | bytes 3408000 | tf_op jit(solution)/shard_map/rcj,rij->cri/dot_general | solution.py:11
  53.2 2.8 %fusion.123 = f32[64,16,128]{2,1,0:T(8,128)S(1)} fusion(f32[64,16,128]{2,1,0:T(8,128)S(1)} %fusion.126, bf16[64,16,128,128]{3,2,1,0:T(8,128)(2,1)} %param.10, bf16[64,16,128]{2,1,0:T(8,128)(2,1)S(1)} %gather_fusion.8, pred[64]{0:T(512)(128)(4,1)S(1)} %get-tuple-element.50, pred[64]{0:T(512)(128)(4,1)S(1)} %get-tuple-element.75), kind=kOutput, calls=%fused_computation.90 | convolution fusion | flops 33947648 | bytes 3408000 | tf_op jit(solution)/shard_map/rcj,rij->cri/dot_general | solution.py:11
  56.0 2.8 %fusion.120 = f32[64,16,128]{2,1,0:T(8,128)S(1)} fusion(f32[64,16,128]{2,1,0:T(8,128)S(1)} %fusion.123, bf16[64,16,128,128]{3,2,1,0:T(8,128)(2,1)} %param.10, bf16[64,16,128]{2,1,0:T(8,128)(2,1)S(1)} %gather_fusion.9, pred[64]{0:T(512)(128)(4,1)S(1)} %get-tuple-element.48, pred[64]{0:T(512)(128)(4,1)S(1)} %get-tuple-element.74), kind=kOutput, calls=%fused_computation.89 | convolution fusion | flops 33947648 | bytes 3408000 | tf_op jit(solution)/shard_map/rcj,rij->cri/dot_general | solution.py:11
  58.9 2.8 %fusion.117 = f32[64,16,128]{2,1,0:T(8,128)S(1)} fusion(f32[64,16,128]{2,1,0:T(8,128)S(1)} %fusion.120, bf16[64,16,128,128]{3,2,1,0:T(8,128)(2,1)} %param.10, bf16[64,16,128]{2,1,0:T(8,128)(2,1)S(1)} %gather_fusion.10, pred[64]{0:T(512)(128)(4,1)S(1)} %get-tuple-element.46, pred[64]{0:T(512)(128)(4,1)S(1)} %get-tuple-element.73), kind=kOutput, calls=%fused_computation.88 | convolution fusion | flops 33947648 | bytes 3408000 | tf_op jit(solution)/shard_map/rcj,rij->cri/dot_general | solution.py:11
  61.7 2.8 %fusion.114 = f32[64,16,128]{2,1,0:T(8,128)S(1)} fusion(f32[64,16,128]{2,1,0:T(8,128)S(1)} %fusion.117, bf16[64,16,128,128]{3,2,1,0:T(8,128)(2,1)} %param.10, bf16[64,16,128]{2,1,0:T(8,128)(2,1)S(1)} %gather_fusion.11, pred[64]{0:T(512)(128)(4,1)S(1)} %get-tuple-element.44, pred[64]{0:T(512)(128)(4,1)S(1)} %get-tuple-element.72), kind=kOutput, calls=%fused_computation.87 | convolution fusion | flops 33947648 | bytes 3408000 | tf_op jit(solution)/shard_map/rcj,rij->cri/dot_general | solution.py:11
  64.6 2.8 %fusion.111 = f32[64,16,128]{2,1,0:T(8,128)S(1)} fusion(f32[64,16,128]{2,1,0:T(8,128)S(1)} %fusion.114, bf16[64,16,128,128]{3,2,1,0:T(8,128)(2,1)} %param.10, bf16[64,16,128]{2,1,0:T(8,128)(2,1)S(1)} %gather_fusion.12, pred[64]{0:T(512)(128)(4,1)S(1)} %get-tuple-element.42, pred[64]{0:T(512)(128)(4,1)S(1)} %get-tuple-element.71), kind=kOutput, calls=%fused_computation.86 | convolution fusion | flops 33947648 | bytes 3408000 | tf_op jit(solution)/shard_map/rcj,rij->cri/dot_general | solution.py:11
  67.4 2.8 %fusion.108 = f32[64,16,128]{2,1,0:T(8,128)S(1)} fusion(f32[64,16,128]{2,1,0:T(8,128)S(1)} %fusion.111, bf16[64,16,128,128]{3,2,1,0:T(8,128)(2,1)} %param.10, bf16[64,16,128]{2,1,0:T(8,128)(2,1)S(1)} %gather_fusion.13, pred[64]{0:T(512)(128)(4,1)S(1)} %get-tuple-element.40, pred[64]{0:T(512)(128)(4,1)S(1)} %get-tuple-element.70), kind=kOutput, calls=%fused_computation.85 | convolution fusion | flops 33947648 | bytes 3408000 | tf_op jit(solution)/shard_map/rcj,rij->cri/dot_general | solution.py:11
  70.3 3.0 %fusion.105 = f32[64,16,128]{2,1,0:T(8,128)S(1)} fusion(f32[64,16,128]{2,1,0:T(8,128)S(1)} %fusion.108, bf16[64,16,128,128]{3,2,1,0:T(8,128)(2,1)} %param.10, bf16[64,16,128]{2,1,0:T(8,128)(2,1)S(1)} %gather_fusion.14, pred[64]{0:T(512)(128)(4,1)S(1)} %get-tuple-element.38, pred[64]{0:T(512)(128)(4,1)S(1)} %get-tuple-element.69), kind=kOutput, calls=%fused_computation.84 | convolution fusion | flops 33947648 | bytes 3408000 | tf_op jit(solution)/shard_map/rcj,rij->cri/dot_general | solution.py:11
  73.3 2.8 %fusion.102 = f32[64,16,128]{2,1,0:T(8,128)S(1)} fusion(f32[64,16,128]{2,1,0:T(8,128)S(1)} %fusion.105, bf16[64,16,128,128]{3,2,1,0:T(8,128)(2,1)} %param.10, bf16[64,16,128]{2,1,0:T(8,128)(2,1)S(1)} %gather_fusion.15, pred[64]{0:T(512)(128)(4,1)S(1)} %get-tuple-element.66, pred[64]{0:T(512)(128)(4,1)S(1)} %get-tuple-element.83), kind=kOutput, calls=%fused_computation.83 | convolution fusion | flops 33947648 | bytes 3408000 | tf_op jit(solution)/shard_map/rcj,rij->cri/dot_general | solution.py:11
  76.1 2.8 %fusion.146 = bf16[16,64,128]{2,0,1:T(8,128)(2,1)S(1)} fusion(f32[64,16,128]{2,1,0:T(8,128)S(1)} %fusion.102, bf16[64,16,128,128]{3,2,1,0:T(8,128)(2,1)} %param.10, bf16[64,16,128]{2,1,0:T(8,128)(2,1)S(1)} %gather_fusion.16, pred[64]{0:T(512)(128)(4,1)S(1)} %get-tuple-element.6, pred[64]{0:T(512)(128)(4,1)S(1)} %get-tuple-element.68), kind=kOutput, calls=%fused_computation.100 | convolution fusion | flops 34078720 | bytes 3145856 | tf_op jit(solution)/shard_map/rcj,rij->cri/dot_general | solution.py:11
  79.0 0.1 copy.86
  79.1 0.2 all_to_all.18
  79.2 0.2 copy.87
  79.4 21.9 %all_to_all.24 = bf16[16,16,512]{2,0,1:T(8,128)(2,1)S(1)} all-to-all(bf16[16,16,512]{2,0,1:T(8,128)(2,1)S(1)} %copy.87), channel_id=1, replica_groups=mesh['vert'=16,'feat'=16] {'feat'}, dimensions={1} | all-to-all | bytes 524288 | tf_op jit(solution)/shard_map/all_to_all | solution.py:33
  101.3 1.0 fusion.145
  (17 shorter events, 0.2 us)
Async XLA Ops:
  0.0 1.4 %copy-start = (bf16[8192,16]{0,1:T(8,128)(2,1)S(1)}, bf16[8192,16]{0,1:T(8,128)(2,1)}, u32[]{:S(2)}) copy-start(bf16[8192,16]{0,1:T(8,128)(2,1)} %param.9) | copy-start | bytes 786436
  1.8 99.5 %copy-start.2 = (f32[256]{0:T(256)S(1)}, f32[256]{0:T(256)}, u32[]{:S(2)}) copy-start(f32[256]{0:T(256)} %param.15) | copy-start | bytes 3076
  3.2 15.0 %all-to-all-start = ((bf16[16,4,16,128]{3,2,1,0:T(8,128)(2,1)}), bf16[16,4,16,128]{3,2,1,0:T(8,128)(2,1)S(1)}, u32[]{:S(2)}, u32[]{:S(2)}) async-start(bf16[16,4,16,128]{3,2,1,0:T(8,128)(2,1)} %broadcast_select_fusion), calls=%async_computation | async-start | bytes 524288 | tf_op jit(solution)/shard_map/all_to_all | solution.py:25
  32.6 68.6 %copy-start.1 = (bf16[256,256]{1,0:T(8,128)(2,1)S(1)}, bf16[256,256]{1,0:T(8,128)(2,1)}, u32[]{:S(2)}) copy-start(bf16[256,256]{1,0:T(8,128)(2,1)} %param.14) | copy-start | bytes 393220
where the time goes:
time: 103 us; the launch traced here: 102 us
  matrix products  47.3 us (46%)
  blocking collectives  21.9 us (21%)
  local copies, waits for them, and re-layouts  15.7 us (15%)
  starting transfers between devices  7.57 us (7%)
  waiting for transfers between devices  5.56 us (5%)
  other arithmetic  4.13 us (4%)
    dot_general x16, matrix products, add_tile(): jnp.einsum('rcj,rij->cri', picked, tile_page, preferred_element_type=jnp....  46.3 us
    all_to_all x1, blocking collectives, per_device(): lax.all_to_all(hidden, 'feat', split_axis=1, concat_axis=0, tiled=True)  21.9 us
    gather x16, local copies, waits for them, and re-layouts, add_tile(): picked = jnp.take(extended, wanted, axis=0)  14.3 us
    all_to_all x1, starting transfers between devices, per_device(): lax.all_to_all(chosen, 'vert', split_axis=0, concat_axis=0, tiled=True)  7.57 us
    all_to_all x1, waiting for transfers between devices, per_device(): lax.all_to_all(chosen, 'vert', split_axis=0, concat_axis=0, tiled=True)  5.56 us
  transfers between devices with their start and end apart: 1, of which 1 were waited for; matrix products, arithmetic and copies ran while one was open for 2% of the time, Pallas kernels for 0%

commit v1 on v0

v1 whole, which is shorter than its diff:
```python
import functools

import jax
import jax.numpy as jnp
from jax import lax
from jax.experimental import pallas as pl
from jax.experimental.pallas import tpu as pltpu
from jax.sharding import PartitionSpec as P

VMEM = pltpu.VMEM
SMEM = pltpu.SMEM
UNROLL = 16
AHEAD = 4
PAIRS_MAX = 8
ROWS = 64
ZERO_SLOT = 64
PAD_ITEM = ((ROWS - 1) << 4) | (ZERO_SLOT << 10) | (ZERO_SLOT << 17)
CHUNKS_MAX = ROWS * PAIRS_MAX // UNROLL
LIST_LEN = ROWS * PAIRS_MAX + PAIRS_MAX + UNROLL + 8


def pick_kernel(send_ref, feat_ref, out_ref):
    slots, peers = send_ref.shape
    for peer in range(peers):
        for slot in range(slots):
            start = pl.multiple_of(send_ref[slot, peer] * 128, 128)
            out_ref[peer * slots + slot] = feat_ref[:, pl.ds(start, 128)]


def run_pairs(list_ref, count, tiles_ref, buf_ref, sem, slab_ref, acc_ref):
    chunks = (count + (UNROLL - 1)) // UNROLL

    def issue(i, carry):
        base = i * UNROLL
        for u in range(UNROLL):
            item = list_ref[base + u]
            ta = item & 1023
            tb = (item & 1008) | (item >> 24)
            at = 2 * (base + u)
            pltpu.make_async_copy(tiles_ref.at[ta], buf_ref.at[at], sem.at[i]).start()
            pltpu.make_async_copy(tiles_ref.at[tb], buf_ref.at[at + 1], sem.at[i]).start()
        return carry

    lax.fori_loop(0, jnp.minimum(chunks, AHEAD), issue, 0)

    def chunk(i, carry):
        base = i * UNROLL
        landed = buf_ref.at[pl.ds(2 * base, 2 * UNROLL)]
        pltpu.make_async_copy(tiles_ref.at[pl.ds(0, 2 * UNROLL)], landed, sem.at[i]).wait()

        @pl.when(i + AHEAD < chunks)
        def _():
            issue(i + AHEAD, 0)

        for u in range(UNROLL):
            item = list_ref[base + u]
            row = (item >> 4) & 63
            xa = (item >> 10) & 127
            xb = (item >> 17) & 127
            at = 2 * (base + u)
            tile = jnp.concatenate([buf_ref[at], buf_ref[at + 1]], axis=1)
            slab = jnp.concatenate([slab_ref[xa], slab_ref[xb]], axis=1)
            acc_ref[row] += lax.dot_general(
                slab, tile, (((1,), (1,)), ((), ())), preferred_element_type=jnp.float32
            )
        return carry

    lax.fori_loop(0, chunks, chunk, 0)


def local_kernel(
    tiles_ref, cols_ref, count_ref, feat_ref,
    acc_ref, halo_ref,
    buf_ref, slab_ref, table_vmem, table_ref, local_ref, load_sem, table_sem,
):
    counts = count_ref[...]
    places = cols_ref.shape[0]
    rank = lax.broadcasted_iota(jnp.int32, (places, ROWS), 0)
    empty = jnp.full((places, ROWS), ZERO_SLOT, jnp.int32)
    codes = [empty, empty]
    seen = [jnp.zeros((1, ROWS), jnp.int32), jnp.zeros((1, ROWS), jnp.int32)]
    for k in range(places):
        col = cols_ref[k:k + 1, :]
        for part in range(2):
            kept = (col < ROWS) if part == 0 else (col >= ROWS)
            kept = kept & (counts > k)
            code = (col - part * ROWS) + (k << 7)
            codes[part] = jnp.where((rank == seen[part]) & kept, code, codes[part])
            seen[part] = seen[part] + kept.astype(jnp.int32)
    rows = lax.broadcasted_iota(jnp.int32, (1, ROWS), 1)
    for part in range(2):
        for p in range(PAIRS_MAX):
            a = codes[part][2 * p:2 * p + 1, :]
            b = codes[part][2 * p + 1:2 * p + 2, :]
            item = (a >> 7) | (rows << 4) | ((a & 127) << 10) | ((b & 127) << 17) | ((b >> 7) << 24)
            at = part * PAIRS_MAX + p
            table_vmem[at:at + 1, 0:ROWS] = item
        at = 2 * PAIRS_MAX + part
        table_vmem[at:at + 1, 0:ROWS] = (seen[part] + 1) >> 1
    to_smem = pltpu.make_async_copy(table_vmem, table_ref, table_sem)
    to_smem.start()

    acc_ref[...] = jnp.zeros(acc_ref.shape, jnp.float32)
    for r in range(ROWS):
        slab_ref[r] = feat_ref[:, r * 128:(r + 1) * 128]
    slab_ref[ZERO_SLOT] = jnp.zeros(slab_ref.shape[1:], slab_ref.dtype)
    to_smem.wait()

    def flatten(part, out_ref):
        def one_row(r, n):
            for p in range(PAIRS_MAX):
                out_ref[n + p] = table_ref[part * PAIRS_MAX + p, r]
            return n + table_ref[2 * PAIRS_MAX + part, r]

        n = lax.fori_loop(0, ROWS, one_row, jnp.int32(0), unroll=2)
        for u in range(UNROLL):
            out_ref[n + u] = PAD_ITEM
        return n

    n_local = flatten(0, local_ref)
    run_pairs(local_ref, n_local, tiles_ref, buf_ref, load_sem, slab_ref, acc_ref)
    halo_ref[LIST_LEN - 1] = flatten(1, halo_ref)


def halo_kernel(
    halo_ref, tiles_ref, part_ref, arrived_ref, out_ref, buf_ref, slab_ref, acc_ref, load_sem
):
    acc_ref[...] = part_ref[...]
    for s in range(arrived_ref.shape[0]):
        slab_ref[s] = arrived_ref[s]
    slab_ref[ZERO_SLOT] = jnp.zeros(slab_ref.shape[1:], slab_ref.dtype)
    n_halo = halo_ref[LIST_LEN - 1]
    run_pairs(halo_ref, n_halo, tiles_ref, buf_ref, load_sem, slab_ref, acc_ref)
    owners = out_ref.shape[0]
    each = ROWS // owners
    for owner in range(owners):
        for j in range(each):
            out_ref[owner, :, j * 128:(j + 1) * 128] = acc_ref[owner * each + j].astype(out_ref.dtype)


def per_device(features, tiles, tile_cols, tile_count, send_list, weight, bias):
    block_count, tile_depth, edge, _ = tiles.shape
    width = features.shape[1]
    feat_count = lax.axis_size("feat")
    bf16, f32 = jnp.bfloat16, jnp.float32
    feat_t = features.T
    whole = pl.BlockSpec(memory_space=VMEM)
    scalar = pl.BlockSpec(memory_space=SMEM)

    chosen = pl.pallas_call(
        pick_kernel,
        out_shape=jax.ShapeDtypeStruct((block_count, width, edge), bf16),
        in_specs=[scalar, whole],
        out_specs=whole,
        name="pick",
        cost_estimate=pl.CostEstimate(flops=1000, bytes_accessed=500000, transcendentals=0),
    )(send_list[0].T, feat_t)
    arrived = lax.all_to_all(
        chosen.reshape(16, 4, width, edge), "vert", split_axis=0, concat_axis=0, tiled=True
    ).reshape(block_count, width, edge)

    flat_tiles = tiles.reshape(block_count * tile_depth, edge, edge)
    in_hbm = pl.BlockSpec(memory_space=pl.ANY)
    buffers = [
        VMEM((2 * UNROLL * CHUNKS_MAX, edge, edge), bf16),
        VMEM((ZERO_SLOT + 1, width, edge), bf16),
    ]
    part, halo = pl.pallas_call(
        local_kernel,
        out_shape=(
            jax.ShapeDtypeStruct((block_count, width, edge), f32),
            jax.ShapeDtypeStruct((LIST_LEN,), jnp.int32),
        ),
        in_specs=[in_hbm, whole, whole, whole],
        out_specs=(whole, scalar),
        scratch_shapes=buffers + [
            VMEM((24, 128), jnp.int32),
            SMEM((24, 128), jnp.int32),
            SMEM((LIST_LEN,), jnp.int32),
            pltpu.SemaphoreType.DMA((CHUNKS_MAX,)),
            pltpu.SemaphoreType.DMA,
        ],
        name="local",
        compiler_params=pltpu.CompilerParams(vmem_limit_bytes=44 * 1024 * 1024),
        cost_estimate=pl.CostEstimate(
            flops=8_000_000_000, bytes_accessed=17_000_000, transcendentals=0
        ),
    )(flat_tiles, tile_cols.T, tile_count.reshape(1, block_count), feat_t)

    hidden = pl.pallas_call(
        halo_kernel,
        out_shape=jax.ShapeDtypeStruct((feat_count, width, block_count * edge // feat_count), bf16),
        in_specs=[scalar, in_hbm, whole, whole],
        out_specs=whole,
        scratch_shapes=buffers + [
            VMEM((block_count, width, edge), f32),
            pltpu.SemaphoreType.DMA((CHUNKS_MAX,)),
        ],
        name="halo",
        compiler_params=pltpu.CompilerParams(vmem_limit_bytes=44 * 1024 * 1024),
        cost_estimate=pl.CostEstimate(
            flops=3_000_000_000, bytes_accessed=17_000_000, transcendentals=0
        ),
    )(halo, flat_tiles, part, arrived)

    full_rows = lax.all_to_all(hidden, "feat", split_axis=0, concat_axis=0, tiled=True)
    full_rows = full_rows.reshape(feat_count * width, -1)
    mixed_rows = lax.dot_general(
        full_rows, weight, (((0,), (0,)), ((), ())), preferred_element_type=f32
    )
    return jnp.maximum(mixed_rows + bias, f32(0.0)).astype(bf16)


def solution(mesh):
    return jax.shard_map(
        per_device,
        mesh=mesh,
        in_specs=(
            P("vert", "feat"),
            P("vert", None, None, None),
            P("vert", None),
            P("vert"),
            P("vert", None, None),
            P(),
            P(),
        ),
        out_specs=P(("vert", "feat"), None),
        check_vma=False,
    )
```

time: 103 us -> 50.4 us (0.49)
  the two profiles are of different devices: /device:TPU:1 before, /device:TPU:23 now
where the time goes in v1:
time: 50.4 us; the launch traced here: 50.2 us
  blocking collectives  21.1 us (42%)
  Pallas kernels  19.1 us (38%)
  starting transfers between devices  6.64 us (13%)
  local copies, waits for them, and re-layouts  2.3 us (5%)
  matrix products  0.98 us (2%)
    all_to_all x1, blocking collectives, per_device(): lax.all_to_all(hidden, 'feat', split_axis=0, concat_axis=0, tiled=True)  21.1 us
    pallas_call x1, Pallas kernels, per_device(): pl.pallas_call(local_kernel, out_shape=(jax.ShapeDtypeStruct((block_count...  9.99 us
    pallas_call x1, Pallas kernels, per_device(): pl.pallas_call(halo_kernel, out_shape=jax.ShapeDtypeStruct((feat_count, w...  7.36 us
    all_to_all x1, starting transfers between devices, per_device(): lax.all_to_all(chosen.reshape(16, 4, width, edge), 'vert', split_axis=0,...  6.64 us
    unnamed x10, local copies, waits for them, and re-layouts  2.3 us
    pallas_call x1, Pallas kernels, per_device(): pl.pallas_call(pick_kernel, out_shape=jax.ShapeDtypeStruct((block_count,...  1.79 us
  transfers between devices with their start and end apart: 1, of which 0 were waited for; matrix products, arithmetic and copies ran while one was open for 0% of the time, Pallas kernels for 20%

profile of v1, /device:TPU:23, one launch (start us, length us, event | category | flops | bytes accessed | tf_op | source)
XLA Modules:
  0.0 50.2 jit_solution(7902808304819573929)
XLA Ops:
  0.0 0.0 copy-start
  0.0 1.8 %pick.1 = bf16[64,16,128]{2,1,0:T(8,128)(2,1)} custom-call(s32[4,16]{1,0:T(4,128)} %bitcast.21, bf16[16,8192]{1,0:T(8,128)(2,1)} %bitcast.12), custom_call_target="tpu_custom_call" | custom-call | flops 1000 | bytes 500000 | tf_op jit(solution)/shard_map/pick/pallas_call | solution.py:150
  1.8 6.6 %all-to-all-start = ((bf16[16,4,16,128]{3,2,1,0:T(8,128)(2,1)}), bf16[16,4,16,128]{3,2,1,0:T(8,128)(2,1)S(1)}, u32[]{:S(2)}, u32[]{:S(2)}) async-start(bf16[16,4,16,128]{3,2,1,0:T(8,128)(2,1)} %bitcast.19), calls=%async_computation | async-start | bytes 524288 | tf_op jit(solution)/shard_map/all_to_all | solution.py:158
  8.4 0.0 copy-start.1
  8.4 0.9 %copy-done.1 = bf16[8192,16]{0,1:T(8,128)(2,1)S(1)} copy-done((bf16[8192,16]{0,1:T(8,128)(2,1)S(1)}, bf16[8192,16]{0,1:T(8,128)(2,1)}, u32[]{:S(2)}) %copy-start.1) | copy-done | bytes 262168
  9.4 0.0 copy-start.2
  9.4 0.7 %copy-done.2 = s32[64,16]{0,1:T(8,128)S(1)} copy-done((s32[64,16]{0,1:T(8,128)S(1)}, s32[64,16]{0,1:T(8,128)}, u32[]{:S(2)}) %copy-start.2) | copy-done | bytes 4120
  10.1 0.0 copy-start.3
  10.1 0.7 %copy-done.3 = s32[64]{0:T(128)S(1)} copy-done((s32[64]{0:T(128)S(1)}, s32[64]{0:T(128)}, u32[]{:S(2)}) %copy-start.3) | copy-done | bytes 280
  10.7 0.0 copy-start.4
  10.7 10.0 %local.1 = (f32[64,16,128]{2,1,0:T(8,128)S(1)}, s32[544]{0:T(1024)S(1)}) custom-call(bf16[1024,128,128]{2,1,0:T(8,128)(2,1)} %bitcast.17, s32[16,64]{1,0:T(8,128)S(1)} %bitcast.15, s32[1,64]{1,0:T(1,128)S(1)} %bitcast.16, bf16[16,8192]{1,0:T(8,128)(2,1)S(1)} %bitcast.13), custom_call_target="tpu_custom_call" | custom-call | flops 8000000000 | bytes 17000000 | tf_op jit(solution)/shard_map/local/pallas_call | solution.py:168
  20.7 0.0 all-to-all-done
  20.7 7.4 %halo.1 = bf16[16,16,512]{2,1,0:T(8,128)(2,1)S(1)} custom-call(s32[544]{0:T(1024)S(1)} %get-tuple-element.7.halo_ref, bf16[1024,128,128]{2,1,0:T(8,128)(2,1)} %bitcast.18, f32[64,16,128]{2,1,0:T(8,128)S(1)} %get-tuple-element.8.part_ref, bf16[64,16,128]{2,1,0:T(8,128)(2,1)S(1)} %bitcast.14), custom_call_target="tpu_custom_call" | custom-call | flops 3000000000 | bytes 17000000 | tf_op jit(solution)/shard_map/halo/pallas_call | solution.py:190
  28.1 21.1 %all_to_all.10 = bf16[16,16,512]{2,1,0:T(8,128)(2,1)S(1)} all-to-all(bf16[16,16,512]{2,1,0:T(8,128)(2,1)S(1)} %halo.1), channel_id=1, replica_groups=mesh['vert'=16,'feat'=16] {'feat'}, dimensions={0} | all-to-all | bytes 524288 | tf_op jit(solution)/shard_map/all_to_all | solution.py:206
  49.2 0.0 copy-done
  49.2 0.0 copy-done.4
  49.2 1.0 %fusion.1 = bf16[512,256]{1,0:T(8,128)(2,1)} fusion(bf16[256,512]{1,0:T(8,128)(2,1)S(1)} %bitcast.20, bf16[256,256]{1,0:T(8,128)(2,1)S(1)} %copy-done, f32[256]{0:T(256)S(1)} %copy-done.4), kind=kOutput, calls=%fused_computation.2 | convolution fusion | flops 67502080 | bytes 656384 | tf_op jit(solution)/shard_map/dot_general | solution.py:208
Async XLA Ops:
  0.0 49.2 %copy-start = (bf16[256,256]{1,0:T(8,128)(2,1)S(1)}, bf16[256,256]{1,0:T(8,128)(2,1)}, u32[]{:S(2)}) copy-start(bf16[256,256]{1,0:T(8,128)(2,1)} %param.12) | copy-start | bytes 393220
  1.8 19.0 %all-to-all-start = ((bf16[16,4,16,128]{3,2,1,0:T(8,128)(2,1)}), bf16[16,4,16,128]{3,2,1,0:T(8,128)(2,1)S(1)}, u32[]{:S(2)}, u32[]{:S(2)}) async-start(bf16[16,4,16,128]{3,2,1,0:T(8,128)(2,1)} %bitcast.19), calls=%async_computation | async-start | bytes 524288 | tf_op jit(solution)/shard_map/all_to_all | solution.py:158
  8.4 0.9 %copy-start.1 = (bf16[8192,16]{0,1:T(8,128)(2,1)S(1)}, bf16[8192,16]{0,1:T(8,128)(2,1)}, u32[]{:S(2)}) copy-start(bf16[8192,16]{0,1:T(8,128)(2,1)} %param.7) | copy-start | bytes 786436
  9.4 0.7 %copy-start.2 = (s32[64,16]{0,1:T(8,128)S(1)}, s32[64,16]{0,1:T(8,128)}, u32[]{:S(2)}) copy-start(s32[64,16]{0,1:T(8,128)} %param.9) | copy-start | bytes 12292
  10.1 0.7 %copy-start.3 = (s32[64]{0:T(128)S(1)}, s32[64]{0:T(128)}, u32[]{:S(2)}) copy-start(s32[64]{0:T(128)} %param.10) | copy-start | bytes 772
  10.7 38.5 %copy-start.4 = (f32[256]{0:T(256)S(1)}, f32[256]{0:T(256)}, u32[]{:S(2)}) copy-start(f32[256]{0:T(256)} %param.13) | copy-start | bytes 3076

commit v2 on v0

v2 whole, which is shorter than its diff:
```python
import jax
import jax.numpy as jnp
from jax import lax
from jax.experimental import pallas as pl
from jax.experimental.pallas import tpu as pltpu
from jax.sharding import PartitionSpec as P

VMEM = pltpu.VMEM
SMEM = pltpu.SMEM
UNROLL = 32
AHEAD = 2
PAIRS_MAX = 8
ROWS = 64
EDGE = 128
SLOTS = ROWS + 1
CHUNKS_MAX = ROWS * PAIRS_MAX // UNROLL
LIST_ROWS = 8
LIST_SPAN = 5 * 128
TOTAL_ROW = 5


def pick_kernel(send_ref, feat_hbm, cols_hbm, count_hbm, out_ref, slab_ref, cols_ref, count_ref, feat_ref, sem):
    copies = [
        pltpu.make_async_copy(src, dst, sem.at[i])
        for i, (src, dst) in enumerate(
            [(feat_hbm, feat_ref), (cols_hbm, cols_ref), (count_hbm, count_ref)]
        )
    ]
    for copy in copies:
        copy.start()
    copies[0].wait()
    slots, peers = send_ref.shape
    for peer in range(peers):
        for slot in range(slots):
            start = pl.multiple_of(send_ref[slot, peer] * EDGE, EDGE)
            out_ref[peer * slots + slot] = feat_ref[:, pl.ds(start, EDGE)]
    slab_ref[0] = jnp.zeros(slab_ref.shape[1:], slab_ref.dtype)
    for r in range(ROWS):
        slab_ref[r + 1] = feat_ref[:, r * EDGE:(r + 1) * EDGE]
    copies[1].wait()
    copies[2].wait()


def item_at(list_ref, i):
    return list_ref[i >> 7, i & 127]


def issue(list_ref, i, tiles_ref, buf_ref, at, sem):
    for u in range(UNROLL):
        item = item_at(list_ref, i * UNROLL + u)
        ta = item & 1023
        tb = (item & 1008) | (item >> 24)
        pltpu.make_async_copy(tiles_ref.at[ta], buf_ref.at[at + 2 * u], sem).start()
        pltpu.make_async_copy(tiles_ref.at[tb], buf_ref.at[at + 2 * u + 1], sem).start()


def landed(tiles_ref, buf_ref, at, sem):
    pltpu.make_async_copy(
        tiles_ref.at[pl.ds(0, 2 * UNROLL)], buf_ref.at[pl.ds(at, 2 * UNROLL)], sem
    ).wait()


def add_chunk(list_ref, i, buf_ref, at, slab_ref, acc_ref):
    for u in range(UNROLL):
        item = item_at(list_ref, i * UNROLL + u)
        row = (item >> 4) & 63
        xa = (item >> 10) & 127
        xb = (item >> 17) & 127
        tile = jnp.concatenate([buf_ref[at + 2 * u], buf_ref[at + 2 * u + 1]], axis=1)
        slab = jnp.concatenate([slab_ref[xa], slab_ref[xb]], axis=1)
        acc_ref[row] += lax.dot_general(
            slab, tile, (((1,), (1,)), ((), ())), preferred_element_type=jnp.float32
        )


def run_chunks(list_ref, first, chunks, tiles_ref, buf_ref, sem, slab_ref, acc_ref):
    def one(i, carry):
        at = i * (2 * UNROLL)
        landed(tiles_ref, buf_ref, at, sem.at[i])

        @pl.when(i + AHEAD < chunks)
        def _():
            issue(list_ref, i + AHEAD, tiles_ref, buf_ref, at + AHEAD * 2 * UNROLL, sem.at[i + AHEAD])

        add_chunk(list_ref, i, buf_ref, at, slab_ref, acc_ref)
        return carry

    lax.fori_loop(first, chunks, one, 0)


def issue_first(list_ref, first, chunks, tiles_ref, buf_ref, sem):
    def one(i, carry):
        issue(list_ref, i, tiles_ref, buf_ref, i * (2 * UNROLL), sem.at[i])
        return carry

    lax.fori_loop(first, jnp.minimum(chunks, first + AHEAD), one, 0)


def chunk_count(list_ref):
    return (list_ref[TOTAL_ROW, 127] + (UNROLL - 1)) // UNROLL


def build_lists(cols_ref, count_ref, piece_ref, halo_table_ref, local_table_ref):
    f32, i32, bf16 = jnp.float32, jnp.int32, jnp.bfloat16
    counts = count_ref[...]
    places = cols_ref.shape[0]
    rank = lax.broadcasted_iota(i32, (places, ROWS), 0)
    codes = [jnp.zeros((places, ROWS), i32)] * 2
    seen = [jnp.zeros((1, ROWS), i32)] * 2
    for k in range(places):
        col = cols_ref[k:k + 1, :]
        for part in range(2):
            kept = (col < ROWS) if part == 0 else (col >= ROWS)
            kept = kept & (counts > k)
            code = (col - part * ROWS + 1) + (k << 7)
            codes[part] = jnp.where((rank == seen[part]) & kept, code, codes[part])
            seen[part] = seen[part] + kept.astype(i32)
    lane_row = lax.broadcasted_iota(i32, (1, ROWS), 1)
    for part in range(2):
        base = part * 32
        for p in range(PAIRS_MAX):
            a = codes[part][2 * p:2 * p + 1, :]
            b = codes[part][2 * p + 1:2 * p + 2, :]
            piece_ref[base + p:base + p + 1, :] = ((a >> 7) | ((b >> 7) << 4)).astype(f32)
            piece_ref[base + 8 + p:base + 9 + p, :] = (a & 127).astype(f32)
            piece_ref[base + 16 + p:base + 17 + p, :] = (b & 127).astype(f32)
        piece_ref[base + 24:base + 25, :] = lane_row.astype(f32)
        piece_ref[base + 25:base + 32, :] = jnp.zeros((7, ROWS), f32)
        piece_ref[64 + part:65 + part, :] = ((seen[part] + 1) >> 1).astype(f32)
    piece_ref[66:72, :] = jnp.zeros((6, ROWS), f32)

    pairs = piece_ref[64:72, :].astype(bf16)
    r_out = lax.broadcasted_iota(i32, (2 * ROWS, ROWS), 0)
    r_in = lax.broadcasted_iota(i32, (2 * ROWS, ROWS), 1)
    before = jnp.where(r_out < ROWS, (r_in < r_out).astype(f32), (r_in == r_out - ROWS).astype(f32))
    nt = (((1,), (1,)), ((), ()))
    nn = (((1,), (0,)), ((), ()))
    column = lax.dot_general(before.astype(bf16), pairs, nt, preferred_element_type=f32)
    spot = lax.broadcasted_iota(i32, (ROWS, LIST_SPAN), 1).astype(f32)
    spot_row = lax.broadcasted_iota(i32, (1, LIST_SPAN), 1)
    p_row = lax.broadcasted_iota(i32, (PAIRS_MAX, LIST_SPAN), 0)
    for part, table_ref in ((0, local_table_ref), (1, halo_table_ref)):
        begin = column[0:ROWS, part:part + 1]
        end = begin + column[ROWS:2 * ROWS, part:part + 1]
        past = spot >= end
        inside = jnp.where((spot >= begin) & jnp.logical_not(past), f32(1), f32(0)).astype(bf16)
        past = jnp.where(past, f32(1), f32(0)).astype(bf16)
        pieces = piece_ref[part * 32:part * 32 + 32, :].astype(bf16)
        chosen = lax.dot_general(pieces, inside, nn, preferred_element_type=f32)
        ahead = lax.dot_general(pairs, past, nn, preferred_element_type=f32)[part:part + 1, :]
        ahead = ahead.astype(i32)
        mine = p_row == (spot_row - ahead)

        def field(at):
            return jnp.sum(
                jnp.where(mine, chosen[at:at + PAIRS_MAX, :], f32(0)), axis=0, keepdims=True
            ).astype(i32)

        place = field(0)
        item = (place & 15) | (chosen[24:25, :].astype(i32) << 4)
        item = item | (field(8) << 10) | (field(16) << 17) | ((place >> 4) << 24)
        for block in range(LIST_SPAN // 128):
            table_ref[block:block + 1, :] = item[:, block * 128:(block + 1) * 128]
        table_ref[TOTAL_ROW:TOTAL_ROW + 1, :] = ahead[:, LIST_SPAN - 128:LIST_SPAN]


def local_kernel(
    tiles_ref, cols_ref, count_ref, slab_ref,
    acc_ref, halo_ref, pre_ref,
    buf_ref, piece_ref, local_vmem, local_list, halo_list, load_sem, pre_sem, list_sem,
):
    build_lists(cols_ref, count_ref, piece_ref, halo_ref, local_vmem)
    to_local = pltpu.make_async_copy(local_vmem, local_list, list_sem.at[0])
    to_halo = pltpu.make_async_copy(halo_ref, halo_list, list_sem.at[1])
    to_local.start()
    to_halo.start()
    acc_ref[...] = jnp.zeros(acc_ref.shape, jnp.float32)
    to_local.wait()
    chunks = chunk_count(local_list)
    issue_first(local_list, 0, chunks, tiles_ref, buf_ref, load_sem)
    to_halo.wait()
    issue(halo_list, 0, tiles_ref, pre_ref, 0, pre_sem)
    run_chunks(local_list, 0, chunks, tiles_ref, buf_ref, load_sem, slab_ref, acc_ref)
    landed(tiles_ref, pre_ref, 0, pre_sem)


def halo_kernel(
    halo_list, tiles_ref, part_ref, pre_ref, arrived_ref, out_ref, buf_ref, slab_ref, acc_ref, load_sem
):
    chunks = chunk_count(halo_list)
    issue_first(halo_list, 1, chunks, tiles_ref, buf_ref, load_sem)
    acc_ref[...] = part_ref[...]
    slab_ref[0] = jnp.zeros(slab_ref.shape[1:], slab_ref.dtype)
    for s in range(ROWS):
        slab_ref[s + 1] = arrived_ref[s]
    add_chunk(halo_list, 0, pre_ref, 0, slab_ref, acc_ref)
    run_chunks(halo_list, 1, chunks, tiles_ref, buf_ref, load_sem, slab_ref, acc_ref)
    owners = out_ref.shape[0]
    each = ROWS // owners
    for owner in range(owners):
        for j in range(each):
            out_ref[owner, :, j * EDGE:(j + 1) * EDGE] = acc_ref[owner * each + j].astype(out_ref.dtype)


def per_device(features, tiles, tile_cols, tile_count, send_list, weight, bias):
    block_count, tile_depth, edge, _ = tiles.shape
    width = features.shape[1]
    feat_count = lax.axis_size("feat")
    vert_count = lax.axis_size("vert")
    bf16, f32, i32 = jnp.bfloat16, jnp.float32, jnp.int32
    whole = pl.BlockSpec(memory_space=VMEM)
    scalar = pl.BlockSpec(memory_space=SMEM)
    in_hbm = pl.BlockSpec(memory_space=pltpu.HBM)
    dma = pltpu.SemaphoreType.DMA
    mib = 1024 * 1024

    chosen, slabs, cols, counts = pl.pallas_call(
        pick_kernel,
        out_shape=(
            jax.ShapeDtypeStruct((block_count, width, edge), bf16),
            VMEM((SLOTS, width, edge), bf16),
            VMEM((tile_depth, block_count), i32),
            VMEM((1, block_count), i32),
        ),
        in_specs=[scalar, in_hbm, in_hbm, in_hbm],
        out_specs=(whole,) * 4,
        scratch_shapes=[VMEM((width, block_count * edge), bf16), dma((3,))],
        name="pick",
        cost_estimate=pl.CostEstimate(flops=1000, bytes_accessed=500000, transcendentals=0),
    )(send_list[0].T, features.T, tile_cols.T, tile_count.reshape(1, block_count))
    arrived = lax.all_to_all(
        chosen.reshape(vert_count, -1, width, edge), "vert", split_axis=0, concat_axis=0, tiled=True
    ).reshape(block_count, width, edge)

    flat_tiles = tiles.reshape(block_count * tile_depth, edge, edge)
    buffer = VMEM((2 * UNROLL * CHUNKS_MAX, edge, edge), bf16)
    part, halo, pre = pl.pallas_call(
        local_kernel,
        out_shape=(
            VMEM((block_count, width, edge), f32),
            VMEM((LIST_ROWS, 128), i32),
            VMEM((2 * UNROLL, edge, edge), bf16),
        ),
        in_specs=[in_hbm, whole, whole, whole],
        out_specs=(whole, whole, whole),
        scratch_shapes=[
            buffer,
            VMEM((72, block_count), f32),
            VMEM((LIST_ROWS, 128), i32),
            SMEM((LIST_ROWS, 128), i32),
            SMEM((LIST_ROWS, 128), i32),
            dma((CHUNKS_MAX,)),
            dma,
            dma((2,)),
        ],
        name="local",
        compiler_params=pltpu.CompilerParams(vmem_limit_bytes=44 * mib),
        cost_estimate=pl.CostEstimate(
            flops=8_000_000_000, bytes_accessed=17_000_000, transcendentals=0
        ),
    )(flat_tiles, cols, counts, slabs)

    hidden = pl.pallas_call(
        halo_kernel,
        out_shape=jax.ShapeDtypeStruct((feat_count, width, block_count * edge // feat_count), bf16),
        in_specs=[scalar, in_hbm, whole, whole, whole],
        out_specs=whole,
        scratch_shapes=[
            buffer,
            VMEM((SLOTS, width, edge), bf16),
            VMEM((block_count, width, edge), f32),
            dma((CHUNKS_MAX,)),
        ],
        name="halo",
        compiler_params=pltpu.CompilerParams(vmem_limit_bytes=44 * mib),
        cost_estimate=pl.CostEstimate(
            flops=3_000_000_000, bytes_accessed=17_000_000, transcendentals=0
        ),
    )(halo, flat_tiles, part, pre, arrived)

    full_rows = lax.all_to_all(hidden, "feat", split_axis=0, concat_axis=0, tiled=True)
    full_rows = full_rows.reshape(feat_count * width, -1)
    mixed_rows = lax.dot_general(
        full_rows, weight, (((0,), (0,)), ((), ())), preferred_element_type=f32
    )
    return jnp.maximum(mixed_rows + bias, f32(0.0)).astype(bf16)


def solution(mesh):
    return jax.shard_map(
        per_device,
        mesh=mesh,
        in_specs=(
            P("vert", "feat"),
            P("vert", None, None, None),
            P("vert", None),
            P("vert"),
            P("vert", None, None),
            P(),
            P(),
        ),
        out_specs=P(("vert", "feat"), None),
        check_vma=False,
    )
```

time: 103 us -> 52.7 us (0.51)
  the two profiles are of different devices: /device:TPU:1 before, /device:TPU:31 now
where the time goes in v2:
time: 52.7 us; the launch traced here: 52.1 us
  Pallas kernels  23.4 us (44%)
  blocking collectives  21.1 us (40%)
  starting transfers between devices  6.54 us (12%)
  matrix products  0.98 us (2%)
    all_to_all x1, blocking collectives, per_device(): lax.all_to_all(hidden, 'feat', split_axis=0, concat_axis=0, tiled=True)  21.1 us
    pallas_call x1, Pallas kernels, per_device(): pl.pallas_call(local_kernel, out_shape=(VMEM((block_count, width, edge),...  11.2 us
    pallas_call x1, Pallas kernels, per_device(): pl.pallas_call(halo_kernel, out_shape=jax.ShapeDtypeStruct((feat_count, w...  9.65 us
    all_to_all x1, starting transfers between devices, per_device(): lax.all_to_all(chosen.reshape(vert_count, -1, width, edge), 'vert', split...  6.54 us
    pallas_call x1, Pallas kernels, per_device(): pl.pallas_call(pick_kernel, out_shape=(jax.ShapeDtypeStruct((block_count,...  2.62 us
  transfers between devices with their start and end apart: 1, of which 0 were waited for; matrix products, arithmetic and copies ran while one was open for 0% of the time, Pallas kernels for 21%

profile of v2, /device:TPU:31, one launch (start us, length us, event | category | flops | bytes accessed | tf_op | source)
XLA Modules:
  0.0 52.1 jit_solution(2297117999544587975)
XLA Ops:
  0.0 0.0 copy-start
  0.0 2.6 %pick.1 = (bf16[64,16,128]{2,1,0:T(8,128)(2,1)}, bf16[65,16,128]{2,1,0:T(8,128)(2,1)S(1)}, s32[16,64]{1,0:T(8,128)S(1)}, s32[1,64]{1,0:T(1,128)S(1)}) custom-call(s32[4,16]{1,0:T(4,128)} %bitcast.19, bf16[16,8192]{1,0:T(8,128)(2,1)} %bitcast.15, s32[16,64]{1,0:T(8,128)} %bitcast.18, s32[1,64]{1,0:T(1,128)} %bitcast.20), custom_call_target="tpu_custom_call" | custom-call | flops 1000 | bytes 500000 | tf_op jit(solution)/shard_map/pick/pallas_call | solution.py:217
  2.6 6.5 %all-to-all-start = ((bf16[16,4,16,128]{3,2,1,0:T(8,128)(2,1)}), bf16[16,4,16,128]{3,2,1,0:T(8,128)(2,1)S(1)}, u32[]{:S(2)}, u32[]{:S(2)}) async-start(bf16[16,4,16,128]{3,2,1,0:T(8,128)(2,1)} %bitcast.16), calls=%async_computation | async-start | bytes 524288 | tf_op jit(solution)/shard_map/all_to_all | solution.py:231
  9.2 0.0 copy-start.1
  9.2 11.2 %local.1 = (f32[64,16,128]{2,1,0:T(8,128)S(1)}, s32[8,128]{1,0:T(8,128)S(1)}, bf16[64,128,128]{2,1,0:T(8,128)(2,1)S(1)}) custom-call(bf16[1024,128,128]{2,1,0:T(8,128)(2,1)} %bitcast.13, s32[16,64]{1,0:T(8,128)S(1)} %get-tuple-element.12.cols_ref, s32[1,64]{1,0:T(1,128)S(1)} %get-tuple-element.13.count_ref, bf16[65,16,128]{2,1,0:T(8,128)(2,1)S(1)} %get-tuple-element.14.slab_ref), custom_call_target="tpu_custom_call" | custom-call | flops 8000000000 | bytes 17000000 | tf_op jit(solution)/shard_map/local/pallas_call | solution.py:237
  20.4 0.0 all-to-all-done
  20.4 9.6 %halo.1 = bf16[16,16,512]{2,1,0:T(8,128)(2,1)S(1)} custom-call(s32[8,128]{1,0:T(8,128)S(1)} %get-tuple-element.15.halo_list, bf16[1024,128,128]{2,1,0:T(8,128)(2,1)} %bitcast.14, f32[64,16,128]{2,1,0:T(8,128)S(1)} %get-tuple-element.16.part_ref, bf16[64,128,128]{2,1,0:T(8,128)(2,1)S(1)} %get-tuple-element.17.pre_ref, bf16[64,16,128]{2,1,0:T(8,128)(2,1)S(1)} %bitcast.12), custom_call_target="tpu_custom_call" | custom-call | flops 3000000000 | bytes 17000000 | tf_op jit(solution)/shard_map/halo/pallas_call | solution.py:263
  30.0 21.1 %all_to_all.10 = bf16[16,16,512]{2,1,0:T(8,128)(2,1)S(1)} all-to-all(bf16[16,16,512]{2,1,0:T(8,128)(2,1)S(1)} %halo.1), channel_id=1, replica_groups=mesh['vert'=16,'feat'=16] {'feat'}, dimensions={0} | all-to-all | bytes 524288 | tf_op jit(solution)/shard_map/all_to_all | solution.py:281
  51.1 0.0 copy-done
  51.1 0.0 copy-done.1
  51.1 1.0 %fusion.1 = bf16[512,256]{1,0:T(8,128)(2,1)} fusion(bf16[256,512]{1,0:T(8,128)(2,1)S(1)} %bitcast.17, bf16[256,256]{1,0:T(8,128)(2,1)S(1)} %copy-done, f32[256]{0:T(256)S(1)} %copy-done.1), kind=kOutput, calls=%fused_computation.2 | convolution fusion | flops 67502080 | bytes 656384 | tf_op jit(solution)/shard_map/dot_general | solution.py:283
Async XLA Ops:
  0.0 51.1 %copy-start = (bf16[256,256]{1,0:T(8,128)(2,1)S(1)}, bf16[256,256]{1,0:T(8,128)(2,1)}, u32[]{:S(2)}) copy-start(bf16[256,256]{1,0:T(8,128)(2,1)} %param.12) | copy-start | bytes 393220
  2.6 17.7 %all-to-all-start = ((bf16[16,4,16,128]{3,2,1,0:T(8,128)(2,1)}), bf16[16,4,16,128]{3,2,1,0:T(8,128)(2,1)S(1)}, u32[]{:S(2)}, u32[]{:S(2)}) async-start(bf16[16,4,16,128]{3,2,1,0:T(8,128)(2,1)} %bitcast.16), calls=%async_computation | async-start | bytes 524288 | tf_op jit(solution)/shard_map/all_to_all | solution.py:231
  9.2 42.0 %copy-start.1 = (f32[256]{0:T(256)S(1)}, f32[256]{0:T(256)}, u32[]{:S(2)}) copy-start(f32[256]{0:T(256)} %param.13) | copy-start | bytes 3076
